TPU v7x, 32 devices: a whole 2x2x4 slice. The times are simulated.
32 devices in a mesh: ctx: 8 (over z, y), dp: 4 (over x, core).
Axes of the slice: x: 2, y: 2, z: 4, core: 2. Of those that a mesh axis runs over, the one named last changes fastest.
Arguments:
- tokens: bfloat16 [8, 512, 4096], P('dp', 'ctx'), may hold values from -6 to 6
- queries: bfloat16 [8, 512, 2048], P('dp', 'ctx'), may hold values from -160 to 160
- d_attended: bfloat16 [8, 512, 2048], P('dp', 'ctx'), may hold values from -6 to 6
- span_order: int32 [16], replicated, may hold values from 0 to 15, each once
- norm_gain: float32 [4096], replicated, may hold values from 0.1 to 1.9
- key_weight: bfloat16 [4096, 512], replicated, may hold values from -0.09375 to 0.09375
- value_weight: bfloat16 [4096, 512], replicated, may hold values from -0.09375 to 0.09375
Outputs:
- attended: bfloat16 [8, 512, 2048], P('dp', 'ctx')
- grad_queries: bfloat16 [8, 512, 2048], P('dp', 'ctx')
- grad_tokens: bfloat16 [8, 512, 4096], P('dp', 'ctx')
- grad_key_weight: float32 [4096, 512], P(('ctx', 'dp'))
- grad_value_weight: float32 [4096, 512], P(('ctx', 'dp'))
- grad_gain: float32 [4096], P(('ctx', 'dp'))
All inputs are finite; a program needn't handle non-finite values.
Results may differ from a plain program's by a relative error of at most 0.025.
The roundings to bfloat16 on the way count: a program that leaves them out, or rounds other values in their place, can miss the bound.
Values may be sent and summed in bfloat16 or wider, within the bound.
A program may use at most 192 MiB of HBM per device.

v0:
```python
import jax
import jax.numpy as jnp
from jax import lax
from jax.sharding import PartitionSpec as P

KV_HEADS = 4
HEAD_DIM = 128
ROPE_BASE = 500000.0
EPSILON = 1e-05


def positions(span_order, span_len):
    offsets = jnp.arange(span_len, dtype=jnp.int32)
    return (span_order[:, None] * span_len + offsets[None, :]).reshape(-1)


def rotation(token_pos, head_size):
    half_dim = head_size // 2
    frequency = ROPE_BASE ** (-2.0 * jnp.arange(half_dim, dtype=jnp.float32) / head_size)
    angles = token_pos.astype(jnp.float32)[:, None] * frequency[None, :]
    angles = jnp.concatenate([angles, angles], axis=1)
    return (jnp.cos(angles), jnp.sin(angles))


def rotate_half(values):
    half_dim = values.shape[-1] // 2
    return jnp.concatenate([-values[..., half_dim:], values[..., :half_dim]], axis=-1)


def rotate_back(values):
    half_dim = values.shape[-1] // 2
    return jnp.concatenate([values[..., half_dim:], -values[..., :half_dim]], axis=-1)


def normalize(tokens, norm_gain):
    widened = tokens.astype(jnp.float32)
    rms_scale = lax.rsqrt(jnp.mean(widened * widened, axis=-1, keepdims=True) + EPSILON)
    return ((widened * rms_scale * norm_gain).astype(jnp.bfloat16), rms_scale)


def project_keys(normed, key_weight, value_weight, cosine, sine_table, kv_heads, head_size):
    row_count = normed.shape[0]
    key_pre = jnp.dot(normed, key_weight, preferred_element_type=jnp.float32).reshape(
        row_count, kv_heads, head_size
    )
    rotated = key_pre * cosine[:, None, :] + rotate_half(key_pre) * sine_table[:, None, :]
    value_rows = jnp.dot(normed, value_weight, preferred_element_type=jnp.float32)
    return (
        rotated.reshape(row_count, kv_heads * head_size).astype(jnp.bfloat16),
        value_rows.astype(jnp.bfloat16),
    )


def attend_group(query_group, grad_group, key_group, value_group, causal_mask, score_scale):
    scores = (
        jnp.einsum("tgd,sd->gts", query_group, key_group, preferred_element_type=jnp.float32)
        * score_scale
    )
    scores = jnp.where(causal_mask[None], scores, -1e30)
    row_max = jnp.max(scores, axis=-1, keepdims=True)
    exponent = jnp.exp(scores - row_max)
    probability = exponent / jnp.sum(exponent, axis=-1, keepdims=True)
    probability_b = probability.astype(jnp.bfloat16)
    attended = jnp.einsum(
        "gts,sd->tgd", probability_b, value_group, preferred_element_type=jnp.float32
    ).astype(jnp.bfloat16)
    dprob = jnp.einsum("tgd,sd->gts", grad_group, value_group, preferred_element_type=jnp.float32)
    delta = jnp.sum(grad_group.astype(jnp.float32) * attended.astype(jnp.float32), axis=-1)
    dscores = (probability * (dprob - jnp.transpose(delta)[:, :, None])).astype(jnp.bfloat16)
    dquery = (
        jnp.einsum("gts,sd->tgd", dscores, key_group, preferred_element_type=jnp.float32)
        * score_scale
    ).astype(jnp.bfloat16)
    key_term = (
        jnp.einsum("gts,tgd->sd", dscores, query_group, preferred_element_type=jnp.float32)
        * score_scale
    )
    value_term = jnp.einsum(
        "gts,tgd->sd", probability_b, grad_group, preferred_element_type=jnp.float32
    )
    return (attended, dquery, key_term, value_term)


def attend_device(queries, grads, all_keys, all_values, query_pos, key_pos, kv_heads, head_size):
    row_count = queries.shape[0]
    group_size = queries.shape[1] // (kv_heads * head_size)
    group_width = group_size * head_size
    causal_mask = key_pos[None, :] <= query_pos[:, None]
    score_scale = head_size ** (-0.5)
    outputs = []
    for head_group in range(kv_heads):
        query_group = queries[:, head_group * group_width : (head_group + 1) * group_width].reshape(
            row_count, group_size, head_size
        )
        grad_group = grads[:, head_group * group_width : (head_group + 1) * group_width].reshape(
            row_count, group_size, head_size
        )
        key_group = all_keys[:, head_group * head_size : (head_group + 1) * head_size]
        value_group = all_values[:, head_group * head_size : (head_group + 1) * head_size]
        outputs.append(
            attend_group(query_group, grad_group, key_group, value_group, causal_mask, score_scale)
        )
    attended = jnp.concatenate(
        [item[0].reshape(row_count, group_width) for item in outputs], axis=1
    )
    dquery = jnp.concatenate([item[1].reshape(row_count, group_width) for item in outputs], axis=1)
    key_terms = jnp.concatenate([item[2] for item in outputs], axis=1)
    value_terms = jnp.concatenate([item[3] for item in outputs], axis=1)
    return (attended, dquery, key_terms, value_terms)


def finish_backward(
    tokens,
    normed,
    rms_scale,
    key_grad,
    value_grad,
    cosine,
    sine_table,
    norm_gain,
    key_weight,
    value_weight,
    kv_heads,
    head_size,
):
    row_count = tokens.shape[0]
    shaped = key_grad.reshape(row_count, kv_heads, head_size)
    key_pre_grad = (
        (shaped * cosine[:, None, :] + rotate_back(shaped * sine_table[:, None, :]))
        .reshape(row_count, kv_heads * head_size)
        .astype(jnp.bfloat16)
    )
    value_pre_grad = value_grad.astype(jnp.bfloat16)
    weight_key = jnp.dot(normed.T, key_pre_grad, preferred_element_type=jnp.float32)
    weight_value = jnp.dot(normed.T, value_pre_grad, preferred_element_type=jnp.float32)
    normed_grad = jnp.dot(key_pre_grad, key_weight.T, preferred_element_type=jnp.float32) + jnp.dot(
        value_pre_grad, value_weight.T, preferred_element_type=jnp.float32
    )
    widened = tokens.astype(jnp.float32)
    gain_part = jnp.sum(normed_grad * widened * rms_scale, axis=0)
    inner_mean = jnp.mean(normed_grad * norm_gain * widened, axis=-1, keepdims=True)
    grad_rows = (
        rms_scale * norm_gain * normed_grad - widened * rms_scale**3 * inner_mean
    ).astype(jnp.bfloat16)
    return (grad_rows, weight_key, weight_value, gain_part)


def body(tokens, queries, d_attended, span_order, norm_gain, key_weight, value_weight):
    local_seqs = tokens.shape[0]
    row_count = tokens.shape[1]
    model_width = tokens.shape[2]
    kv_width = key_weight.shape[1]
    shard_index = lax.axis_index("ctx")
    token_pos = positions(span_order, row_count // 2)
    query_pos = lax.dynamic_slice_in_dim(token_pos, shard_index * row_count, row_count, 0)
    cosine, sine_table = rotation(query_pos, HEAD_DIM)
    cosine_all = jnp.tile(cosine, (local_seqs, 1))
    sine_all = jnp.tile(sine_table, (local_seqs, 1))
    flat_tokens = tokens.reshape(local_seqs * row_count, model_width)
    normed, rms_scale = normalize(flat_tokens, norm_gain)
    rotated_keys, value_rows = project_keys(
        normed, key_weight, value_weight, cosine_all, sine_all, KV_HEADS, HEAD_DIM
    )
    rotated_keys = rotated_keys.reshape(local_seqs, row_count, kv_width)
    value_rows = value_rows.reshape(local_seqs, row_count, kv_width)
    all_keys, all_values = (
        lax.all_gather(rotated_keys, "ctx", axis=1, tiled=True),
        lax.all_gather(value_rows, "ctx", axis=1, tiled=True),
    )
    attended_list, dquery_list, key_list, value_list = ([], [], [], [])
    for sequence in range(local_seqs):
        attended, dquery, key_terms, value_terms = attend_device(
            queries[sequence],
            d_attended[sequence],
            all_keys[sequence],
            all_values[sequence],
            query_pos,
            token_pos,
            KV_HEADS,
            HEAD_DIM,
        )
        attended_list.append(attended)
        dquery_list.append(dquery)
        key_list.append(key_terms)
        value_list.append(value_terms)
    key_stack = jnp.stack(key_list)
    value_stack = jnp.stack(value_list)
    key_grad, value_grad = (
        lax.psum_scatter(
            key_stack.astype(jnp.bfloat16), "ctx", scatter_dimension=1, tiled=True
        ).astype(jnp.float32),
        lax.psum_scatter(
            value_stack.astype(jnp.bfloat16), "ctx", scatter_dimension=1, tiled=True
        ).astype(jnp.float32),
    )
    key_grad = key_grad.reshape(local_seqs * row_count, kv_width)
    value_grad = value_grad.reshape(local_seqs * row_count, kv_width)
    grad_rows, weight_key, weight_value, gain_part = finish_backward(
        flat_tokens,
        normed,
        rms_scale,
        key_grad,
        value_grad,
        cosine_all,
        sine_all,
        norm_gain,
        key_weight,
        value_weight,
        KV_HEADS,
        HEAD_DIM,
    )
    weight_key, weight_value, gain_part = (
        lax.psum_scatter(
            weight_key.astype(jnp.bfloat16), "ctx", scatter_dimension=0, tiled=True
        ).astype(jnp.float32),
        lax.psum_scatter(
            weight_value.astype(jnp.bfloat16), "ctx", scatter_dimension=0, tiled=True
        ).astype(jnp.float32),
        lax.psum_scatter(
            gain_part.astype(jnp.bfloat16), "ctx", scatter_dimension=0, tiled=True
        ).astype(jnp.float32),
    )
    weight_key, weight_value, gain_part = (
        lax.psum_scatter(
            weight_key.astype(jnp.bfloat16), "dp", scatter_dimension=0, tiled=True
        ).astype(jnp.float32),
        lax.psum_scatter(
            weight_value.astype(jnp.bfloat16), "dp", scatter_dimension=0, tiled=True
        ).astype(jnp.float32),
        lax.psum_scatter(
            gain_part.astype(jnp.bfloat16), "dp", scatter_dimension=0, tiled=True
        ).astype(jnp.float32),
    )
    return (
        jnp.stack(attended_list),
        jnp.stack(dquery_list),
        grad_rows.reshape(local_seqs, row_count, model_width),
        weight_key,
        weight_value,
        gain_part,
    )


def solution(mesh):
    placed = (P("dp", "ctx", None), P("dp", "ctx", None), P("dp", "ctx", None), P(), P(), P(), P())
    return jax.shard_map(
        body,
        mesh=mesh,
        in_specs=placed,
        out_specs=(
            P("dp", "ctx", None),
            P("dp", "ctx", None),
            P("dp", "ctx", None),
            P(("ctx", "dp"), None),
            P(("ctx", "dp"), None),
            P(("ctx", "dp")),
        ),
        check_vma=False,
    )
```

profile of v0, /device:TPU:0, one launch (start us, length us, event | category | flops | bytes accessed | tf_op | source)
XLA Modules:
  0.0 512.8 jit_solution(5786807104449921285)
XLA Ops:
  10.2 6.5 %copy.154 = bf16[512,4096]{1,0:T(8,128)(2,1)} copy(bf16[512,4096]{0,1:T(8,128)(2,1)} %bitcast.753) | data formatting | bytes 8388608 | tf_op jit(solution)/shard_map/dot_general | solution.py:43
  17.0 3.4 fusion.276
  21.9 3.7 convolution_convert_fusion.1
  27.7 36.9 %all-gather.5.cloned.1.call-done = bf16[2,512,512]{2,1,0:T(8,128)(2,1)} async-done(((bf16[2,64,512]{2,1,0:T(8,128)(2,1)}), bf16[2,512,512]{2,1,0:T(8,128)(2,1)}) %all-gather.5.cloned.1.call-update) | async-done | bytes 1048592 | tf_op jit(solution)/shard_map/all_gather | solution.py:167
  70.5 35.8 %all-gather.3.cloned.1.call-done = bf16[2,512,512]{2,1,0:T(8,128)(2,1)} async-done(((bf16[2,64,512]{2,1,0:T(8,128)(2,1)}), bf16[2,512,512]{2,1,0:T(8,128)(2,1)}) %all-gather.3.cloned.1.call-update) | async-done | bytes 1048592 | tf_op jit(solution)/shard_map/all_gather | solution.py:168
  113.6 2.4 multiply_reduce_fusion.5
  120.6 2.4 multiply_reduce_fusion.6
  123.9 2.4 fusion.273
  127.5 2.4 multiply_reduce_fusion.7
  130.8 2.5 fusion.252
  136.8 2.5 fusion.255
  142.8 2.4 fusion.258
  163.6 2.1 copy.150
  168.1 2.1 copy.137
  172.1 99.3 %all-reduce.7.cloned.1.call-done = (bf16[2,512,512]{2,0,1:T(2,128)(2,1)}, bf16[2,512,512]{2,0,1:T(2,128)(2,1)}) async-done(((bf16[2,512,512]{2,0,1:T(2,128)(2,1)}, bf16[2,512,512]{2,0,1:T(2,128)(2,1)}), (bf16[2,512,512]{2,0,1:T(2,128)(2,1)}, bf16[2,512,512]{2,0,1:T(2,128)(2,1)})) %all-reduce.7.cloned.1.call-update) | async-done | bytes 2097168
  273.4 3.2 convolution_convert_fusion
  277.8 3.3 bitcast_convert_fusion
  295.8 68.7 %reduce-scatter.5.cloned.1.call-done = bf16[512,512]{1,0:T(8,128)(2,1)} async-done(((bf16[4096,512]{1,0:T(8,128)(2,1)}), bf16[512,512]{1,0:T(8,128)(2,1)}) %reduce-scatter.5.cloned.1.call-update) | async-done | bytes 524304 | tf_op jit(solution)/shard_map/reduce_scatter | solution.py:213
  364.6 3.8 fusion.277
  370.2 21.3 %all-reduce.2 = bf16[4096]{0:T(1024)(128)(2,1)S(1)} all-reduce(bf16[4096]{0:T(1024)(128)(2,1)S(1)} %get-tuple-element.6), channel_id=8, replica_groups=mesh['ctx'=8,'dp'=4] {'ctx'}, use_global_device_ids=true, to_apply=%region_33.34.clone | all-reduce | flops 4096 | bytes 16384
  391.6 6.0 %all-reduce.3 = bf16[512]{0:T(512)(128)(2,1)S(1)} all-reduce(bf16[512]{0:T(512)(128)(2,1)S(1)} %dynamic-slice.5), channel_id=9, replica_groups=mesh['ctx'=8,'dp'=4] {'dp'}, use_global_device_ids=true, to_apply=%region_34.35.clone | all-reduce | flops 512 | bytes 2048
  397.7 58.8 %reduce-scatter.9.cloned.1.call-done = bf16[512,512]{1,0:T(8,128)(2,1)} async-done(((bf16[4096,512]{1,0:T(8,128)(2,1)}), bf16[512,512]{1,0:T(8,128)(2,1)}) %reduce-scatter.9.cloned.1.call-update) | async-done | bytes 524304 | tf_op jit(solution)/shard_map/reduce_scatter | solution.py:216
  458.7 21.4 %reduce-scatter.7.cloned.1.call-done = bf16[128,512]{1,0:T(8,128)(2,1)} async-done(((bf16[512,512]{1,0:T(8,128)(2,1)}), bf16[128,512]{1,0:T(8,128)(2,1)}) %reduce-scatter.7.cloned.1.call-update) | async-done | bytes 131088 | tf_op jit(solution)/shard_map/reduce_scatter | solution.py:224
  481.7 22.5 %reduce-scatter.11.cloned.1.call-done = bf16[128,512]{1,0:T(8,128)(2,1)} async-done(((bf16[512,512]{1,0:T(8,128)(2,1)}), bf16[128,512]{1,0:T(8,128)(2,1)}) %reduce-scatter.11.cloned.1.call-update) | async-done | bytes 131088 | tf_op jit(solution)/shard_map/reduce_scatter | solution.py:227
  (343 shorter events, 79.2 us)
Async XLA Ops:
  7.2 57.4 %all-gather.5.cloned.1.call-start = ((), (), s32[]{:S(2)}) async-start(), calls=%async_computation.5 | async-start | bytes 1179648 | tf_op jit(solution)/shard_map/all_gather | solution.py:167
  21.4 84.9 %all-gather.3.cloned.1.call-start = ((), (), s32[]{:S(2)}) async-start(), calls=%async_computation.4 | async-start | bytes 1179648 | tf_op jit(solution)/shard_map/all_gather | solution.py:168
  25.6 245.8 %all-reduce.7.cloned.1.call-start = ((), (), s32[]{:S(2)}) async-start(), calls=%async_computation.10 | async-start | bytes 4194304
  26.7 39.2 %copy-start.69 = (bf16[8,4,8,128]{3,2,1,0:T(8,128)(2,1)}, bf16[8,4,8,128]{3,2,1,0:T(8,128)(2,1)S(1)}, u32[]{:S(2)}) copy-start(bf16[8,4,8,128]{3,2,1,0:T(8,128)(2,1)S(1)} %get-tuple-element.83) | copy-start | bytes 196612
  26.8 39.1 %copy-start.79 = (pred[64,512]{1,0:T(8,128)(4,1)}, pred[64,512]{1,0:T(8,128)(4,1)S(1)}, u32[]{:S(2)}) copy-start(pred[64,512]{1,0:T(8,128)(4,1)S(1)} %broadcast_compare_fusion) | copy-start | bytes 98308
  65.8 58.0 %copy-start.4 = (bf16[512,512]{1,0:T(8,128)(2,1)}, bf16[512,512]{1,0:T(8,128)(2,1)S(1)}, u32[]{:S(2)}) copy-start(bf16[512,512]{1,0:T(8,128)(2,1)S(1)} %get-tuple-element.14) | copy-start | bytes 1572868
  65.8 82.9 %copy-start.2 = (bf16[512,512]{1,0:T(8,128)(2,1)}, bf16[512,512]{1,0:T(8,128)(2,1)S(1)}, u32[]{:S(2)}) copy-start(bf16[512,512]{1,0:T(8,128)(2,1)S(1)} %get-tuple-element.15) | copy-start | bytes 1572868
  111.8 8.8 %copy-start.29 = (bf16[8,4,8,128]{3,2,1,0:T(8,128)(2,1)S(1)}, bf16[8,4,8,128]{3,2,1,0:T(8,128)(2,1)}, u32[]{:S(2)}) copy-start(bf16[8,4,8,128]{3,2,1,0:T(8,128)(2,1)} %get-tuple-element.77) | copy-start | bytes 196612
  113.5 10.3 %copy-start.65 = (bf16[8,4,8,128]{3,2,1,0:T(8,128)(2,1)S(1)}, bf16[8,4,8,128]{3,2,1,0:T(8,128)(2,1)}, u32[]{:S(2)}) copy-start(bf16[8,4,8,128]{3,2,1,0:T(8,128)(2,1)} %get-tuple-element.84) | copy-start | bytes 196612
  118.8 8.7 %copy-start.27 = (bf16[8,4,8,128]{3,2,1,0:T(8,128)(2,1)S(1)}, bf16[8,4,8,128]{3,2,1,0:T(8,128)(2,1)}, u32[]{:S(2)}) copy-start(bf16[8,4,8,128]{3,2,1,0:T(8,128)(2,1)} %get-tuple-element.80) | copy-start | bytes 196612
  120.5 10.2 %copy-start.63 = (bf16[8,4,8,128]{3,2,1,0:T(8,128)(2,1)S(1)}, bf16[8,4,8,128]{3,2,1,0:T(8,128)(2,1)}, u32[]{:S(2)}) copy-start(bf16[8,4,8,128]{3,2,1,0:T(8,128)(2,1)} %get-tuple-element.37) | copy-start | bytes 196612
  126.3 8.1 %copy-start.25 = (bf16[8,4,8,128]{3,2,1,0:T(8,128)(2,1)S(1)}, bf16[8,4,8,128]{3,2,1,0:T(8,128)(2,1)}, u32[]{:S(2)}) copy-start(bf16[8,4,8,128]{3,2,1,0:T(8,128)(2,1)} %get-tuple-element.29) | copy-start | bytes 196612
  126.3 9.1 %copy-start.6 = (bf16[512,512]{1,0:T(8,128)(2,1)S(1)}, bf16[512,512]{1,0:T(8,128)(2,1)}, u32[]{:S(2)}) copy-start(bf16[512,512]{1,0:T(8,128)(2,1)} %get-tuple-element.13) | copy-start | bytes 1572868
  127.5 9.3 %copy-start.61 = (bf16[8,4,8,128]{3,2,1,0:T(8,128)(2,1)S(1)}, bf16[8,4,8,128]{3,2,1,0:T(8,128)(2,1)}, u32[]{:S(2)}) copy-start(bf16[8,4,8,128]{3,2,1,0:T(8,128)(2,1)} %get-tuple-element.38) | copy-start | bytes 196612
  133.2 7.2 %copy-start.23 = (bf16[8,4,8,128]{3,2,1,0:T(8,128)(2,1)S(1)}, bf16[8,4,8,128]{3,2,1,0:T(8,128)(2,1)}, u32[]{:S(2)}) copy-start(bf16[8,4,8,128]{3,2,1,0:T(8,128)(2,1)} %get-tuple-element.30) | copy-start | bytes 196612
  134.4 8.4 %copy-start.59 = (bf16[8,4,8,128]{3,2,1,0:T(8,128)(2,1)S(1)}, bf16[8,4,8,128]{3,2,1,0:T(8,128)(2,1)}, u32[]{:S(2)}) copy-start(bf16[8,4,8,128]{3,2,1,0:T(8,128)(2,1)} %get-tuple-element.39) | copy-start | bytes 196612
  139.3 7.2 %copy-start.21 = (bf16[8,4,8,128]{3,2,1,0:T(8,128)(2,1)S(1)}, bf16[8,4,8,128]{3,2,1,0:T(8,128)(2,1)}, u32[]{:S(2)}) copy-start(bf16[8,4,8,128]{3,2,1,0:T(8,128)(2,1)} %get-tuple-element.31) | copy-start | bytes 196612
  140.4 8.3 %copy-start.57 = (bf16[8,4,8,128]{3,2,1,0:T(8,128)(2,1)S(1)}, bf16[8,4,8,128]{3,2,1,0:T(8,128)(2,1)}, u32[]{:S(2)}) copy-start(bf16[8,4,8,128]{3,2,1,0:T(8,128)(2,1)} %get-tuple-element.36) | copy-start | bytes 196612
  170.2 194.3 %reduce-scatter.5.cloned.1.call-start = ((), (), s32[]{:S(2)}) async-start(), calls=%async_computation.6 | async-start | bytes 4718592 | tf_op jit(solution)/shard_map/reduce_scatter | solution.py:213
  276.7 179.8 %reduce-scatter.9.cloned.1.call-start = ((), (), s32[]{:S(2)}) async-start(), calls=%async_computation.8 | async-start | bytes 4718592 | tf_op jit(solution)/shard_map/reduce_scatter | solution.py:216
  281.1 7.6 %copy-start.3 = (bf16[512,512]{1,0:T(8,128)(2,1)S(1)}, bf16[512,512]{1,0:T(8,128)(2,1)}, u32[]{:S(2)}) copy-start(bf16[512,512]{1,0:T(8,128)(2,1)} %copy-done.2) | copy-start | bytes 1572868
  281.1 199.0 %reduce-scatter.7.cloned.1.call-start = ((), (), s32[]{:S(2)}) async-start(), calls=%async_computation.7 | async-start | bytes 655360 | tf_op jit(solution)/shard_map/reduce_scatter | solution.py:224
  364.6 139.7 %reduce-scatter.11.cloned.1.call-start = ((), (), s32[]{:S(2)}) async-start(), calls=%async_computation.9 | async-start | bytes 655360 | tf_op jit(solution)/shard_map/reduce_scatter | solution.py:227
  368.5 88.6 %copy-start.98 = (f32[128]{0:T(128)S(1)}, f32[128]{0:T(128)}, u32[]{:S(2)}) copy-start(f32[128]{0:T(128)} %multiply_multiply_fusion) | copy-start | bytes 1540
  (84 other events, 258.2 us)
Sparse Core Ops, SparseCore 0:
  21.6 42.9 all-gather.4
  67.3 38.9 all-gather.2
  170.3 101.0 all-reduce.6
  276.8 87.6 reduce-scatter.4
  368.0 88.4 reduce-scatter.8
  458.8 21.2 reduce-scatter.6
  482.6 21.6 reduce-scatter.10
where the time goes:
time: 514 us; the launch traced here: 513 us
  waiting for transfers between devices  344 us (67%)
  matrix products  75.4 us (15%)
  blocking collectives  27.4 us (5%)
  local copies, waits for them, and re-layouts  26.2 us (5%)
  other arithmetic  21.8 us (4%)
  between operations  17.6 us (3%)
    unnamed x8, waiting for transfers between devices  99.4 us
    reduce_scatter x1, waiting for transfers between devices, body(): lax.psum_scatter(weight_key.astype(jnp.bfloat16), 'ctx', scatter_dimensio...  68.7 us
    reduce_scatter x1, waiting for transfers between devices, body(): lax.psum_scatter(weight_value.astype(jnp.bfloat16), 'ctx', scatter_dimens...  58.8 us
    all_gather x1, waiting for transfers between devices, body(): lax.all_gather(rotated_keys, 'ctx', axis=1, tiled=True)  36.9 us
    all_gather x1, waiting for transfers between devices, body(): lax.all_gather(value_rows, 'ctx', axis=1, tiled=True)  35.8 us
    unnamed x2, blocking collectives  27.4 us
    reduce_scatter x1, waiting for transfers between devices, body(): lax.psum_scatter(weight_value.astype(jnp.bfloat16), 'dp', scatter_dimensi...  22.5 us
    reduce_scatter x1, waiting for transfers between devices, body(): lax.psum_scatter(weight_key.astype(jnp.bfloat16), 'dp', scatter_dimension...  21.4 us
  transfers between devices with their start and end apart: 7, of which 7 were waited for; matrix products, arithmetic and copies ran while one was open for 8% of the time, Pallas kernels for 0%

commit v1 on v0

--- a/solution.py
+++ b/solution.py
@@ -1,3 +1,4 @@
+import functools
 import jax
 import jax.numpy as jnp
 from jax import lax
@@ -7,6 +8,18 @@
 HEAD_DIM = 128
 ROPE_BASE = 500000.0
 EPSILON = 1e-05
+
+
+def do_task(local, comm_axis):
+    return jnp.concatenate(
+        lax.all_to_all(
+            jnp.stack(tuple((local for _ in range(lax.axis_size(comm_axis))))), comm_axis, 0, 0
+        ),
+        axis=1,
+    )
+
+
+link_object = functools.partial(do_task, comm_axis="ctx")
 
 
 def positions(span_order, span_len):
@@ -165,7 +178,7 @@
     value_rows = value_rows.reshape(local_seqs, row_count, kv_width)
     all_keys, all_values = (
         lax.all_gather(rotated_keys, "ctx", axis=1, tiled=True),
-        lax.all_gather(value_rows, "ctx", axis=1, tiled=True),
+        link_object(value_rows),
     )
     attended_list, dquery_list, key_list, value_list = ([], [], [], [])
     for sequence in range(local_seqs):

time: 514 us -> 493 us (0.959)
  waiting for transfers between devices: 344 us -> 304 us
  starting transfers between devices: 0.69 us -> 8.08 us
    all_gather x1 -> x0, waiting for transfers between devices: 35.8 us -> none  [body(): lax.all_gather(value_rows, 'ctx', axis=1, tiled=True)]
    all_gather x1, waiting for transfers between devices: 36.9 us -> 27.5 us  [body(): lax.all_gather(rotated_keys, 'ctx', axis=1, tiled=True)]
    all_to_all x0 -> x1, waiting for transfers between devices: none -> 9.04 us  [do_task(): lax.all_to_all(jnp.stack(tuple((local for _ in range(lax.axis_size(comm_a...]
    all_to_all x0 -> x1, starting transfers between devices: none -> 7.44 us  [do_task(): lax.all_to_all(jnp.stack(tuple((local for _ in range(lax.axis_size(comm_a...]
    unnamed x8 -> x7, waiting for transfers between devices: 99.4 us -> 99.4 us
  transfers between devices with their start and end apart: 7 -> 7, of which waited for: 7 -> 7; matrix products, arithmetic and copies ran while one was open for 8% -> 10% of each run, Pallas kernels for 0% -> 0%
where the time goes in v1:
time: 493 us; the launch traced here: 491 us
  waiting for transfers between devices  304 us (62%)
  matrix products  80.2 us (16%)
  local copies, waits for them, and re-layouts  28 us (6%)
  blocking collectives  27.7 us (6%)
  other arithmetic  25.7 us (5%)
  between operations  17.6 us (4%)
  starting transfers between devices  8.08 us (2%)
    unnamed x7, waiting for transfers between devices  99.4 us
    reduce_scatter x1, waiting for transfers between devices, body(): lax.psum_scatter(weight_key.astype(jnp.bfloat16), 'ctx', scatter_dimensio...  68.7 us
    reduce_scatter x1, waiting for transfers between devices, body(): lax.psum_scatter(weight_value.astype(jnp.bfloat16), 'ctx', scatter_dimens...  57.3 us
    unnamed x2, blocking collectives  27.7 us
    all_gather x1, waiting for transfers between devices, body(): lax.all_gather(rotated_keys, 'ctx', axis=1, tiled=True)  27.5 us
    reduce_scatter x1, waiting for transfers between devices, body(): lax.psum_scatter(weight_value.astype(jnp.bfloat16), 'dp', scatter_dimensi...  22.4 us
    reduce_scatter x1, waiting for transfers between devices, body(): lax.psum_scatter(weight_key.astype(jnp.bfloat16), 'dp', scatter_dimension...  19.8 us
    sub x8, matrix products, attend_group(): exponent = jnp.exp(scores - row_max)  18.5 us
  transfers between devices with their start and end apart: 7, of which 7 were waited for; matrix products, arithmetic and copies ran while one was open for 10% of the time, Pallas kernels for 0%

profile of v1, /device:TPU:0, one launch (start us, length us, event | category | flops | bytes accessed | tf_op | source)
XLA Modules:
  0.0 491.5 jit_solution(4994864303051592058)
XLA Ops:
  10.9 2.9 convolution_convert_fusion.1
  14.9 7.4 %all-to-all-start = ((bf16[8,2,64,512]{3,2,1,0:T(8,128)(2,1)}), bf16[8,2,64,512]{3,2,1,0:T(8,128)(2,1)S(1)}, u32[]{:S(2)}, u32[]{:S(2)}) async-start(bf16[8,2,64,512]{3,2,1,0:T(8,128)(2,1)} %stack.45), calls=%async_computation | async-start | bytes 2097152 | tf_op jit(solution)/shard_map/all_to_all | solution.py:15
  24.1 6.4 %copy.154 = bf16[512,4096]{1,0:T(8,128)(2,1)} copy(bf16[512,4096]{0,1:T(8,128)(2,1)} %bitcast.752) | data formatting | bytes 8388608 | tf_op jit(solution)/shard_map/dot_general | solution.py:56
  30.5 3.4 fusion.277
  39.3 9.0 %all-to-all-done = bf16[8,2,64,512]{3,2,1,0:T(8,128)(2,1)S(1)} async-done(((bf16[8,2,64,512]{3,2,1,0:T(8,128)(2,1)}), bf16[8,2,64,512]{3,2,1,0:T(8,128)(2,1)S(1)}, u32[]{:S(2)}, u32[]{:S(2)}) %all-to-all-start) | async-done | bytes 1048608 | tf_op jit(solution)/shard_map/all_to_all | solution.py:15
  49.4 27.5 %all-gather.2.cloned.1.call-done = bf16[2,512,512]{2,1,0:T(8,128)(2,1)} async-done(((bf16[2,64,512]{2,1,0:T(8,128)(2,1)}), bf16[2,512,512]{2,1,0:T(8,128)(2,1)}) %all-gather.2.cloned.1.call-update) | async-done | bytes 1048592 | tf_op jit(solution)/shard_map/all_gather | solution.py:180
  78.1 2.6 fusion.265
  85.9 2.5 fusion.268
  89.6 2.3 multiply_reduce_fusion.5
  93.7 2.5 fusion.271
  101.4 2.5 fusion.274
  109.1 2.5 fusion.253
  150.8 99.3 %all-reduce.7.cloned.1.call-done = (bf16[2,512,512]{2,0,1:T(2,128)(2,1)}, bf16[2,512,512]{2,0,1:T(2,128)(2,1)}) async-done(((bf16[2,512,512]{2,0,1:T(2,128)(2,1)}, bf16[2,512,512]{2,0,1:T(2,128)(2,1)}), (bf16[2,512,512]{2,0,1:T(2,128)(2,1)}, bf16[2,512,512]{2,0,1:T(2,128)(2,1)})) %all-reduce.7.cloned.1.call-update) | async-done | bytes 2097168
  252.2 3.3 convolution_convert_fusion
  256.6 3.3 bitcast_convert_fusion
  274.6 68.7 %reduce-scatter.5.cloned.1.call-done = bf16[512,512]{1,0:T(8,128)(2,1)} async-done(((bf16[4096,512]{1,0:T(8,128)(2,1)}), bf16[512,512]{1,0:T(8,128)(2,1)}) %reduce-scatter.5.cloned.1.call-update) | async-done | bytes 524304 | tf_op jit(solution)/shard_map/reduce_scatter | solution.py:226
  343.3 3.8 fusion.278
  347.2 3.0 fusion.18
  350.2 21.7 %all-reduce.2 = bf16[4096]{0:T(1024)(128)(2,1)S(1)} all-reduce(bf16[4096]{0:T(1024)(128)(2,1)S(1)} %get-tuple-element.6), channel_id=8, replica_groups=mesh['ctx'=8,'dp'=4] {'ctx'}, use_global_device_ids=true, to_apply=%region_33.34.clone | all-reduce | flops 4096 | bytes 16384
  372.0 6.0 %all-reduce.3 = bf16[512]{0:T(512)(128)(2,1)S(1)} all-reduce(bf16[512]{0:T(512)(128)(2,1)S(1)} %dynamic-slice.5), channel_id=9, replica_groups=mesh['ctx'=8,'dp'=4] {'dp'}, use_global_device_ids=true, to_apply=%region_34.35.clone | all-reduce | flops 512 | bytes 2048
  378.0 57.3 %reduce-scatter.9.cloned.1.call-done = bf16[512,512]{1,0:T(8,128)(2,1)} async-done(((bf16[4096,512]{1,0:T(8,128)(2,1)}), bf16[512,512]{1,0:T(8,128)(2,1)}) %reduce-scatter.9.cloned.1.call-update) | async-done | bytes 524304 | tf_op jit(solution)/shard_map/reduce_scatter | solution.py:229
  435.9 3.2 fusion.15
  439.1 19.8 %reduce-scatter.7.cloned.1.call-done = bf16[128,512]{1,0:T(8,128)(2,1)} async-done(((bf16[512,512]{1,0:T(8,128)(2,1)}), bf16[128,512]{1,0:T(8,128)(2,1)}) %reduce-scatter.7.cloned.1.call-update) | async-done | bytes 131088 | tf_op jit(solution)/shard_map/reduce_scatter | solution.py:237
  460.6 22.4 %reduce-scatter.11.cloned.1.call-done = bf16[128,512]{1,0:T(8,128)(2,1)} async-done(((bf16[512,512]{1,0:T(8,128)(2,1)}), bf16[128,512]{1,0:T(8,128)(2,1)}) %reduce-scatter.11.cloned.1.call-update) | async-done | bytes 131088 | tf_op jit(solution)/shard_map/reduce_scatter | solution.py:240
  (323 shorter events, 90.3 us)
Async XLA Ops:
  13.8 8.6 %copy-start = (bf16[2,64,4096]{2,1,0:T(8,128)(2,1)S(1)}, bf16[2,64,4096]{2,1,0:T(8,128)(2,1)}, u32[]{:S(2)}) copy-start(bf16[2,64,4096]{2,1,0:T(8,128)(2,1)} %param.7) | copy-start | bytes 3145732
  13.8 8.6 %copy-start.50 = (f32[4096]{0:T(1024)S(1)}, f32[4096]{0:T(1024)}, u32[]{:S(2)}) copy-start(f32[4096]{0:T(1024)} %param.11) | copy-start | bytes 49156
  14.9 7.9 %copy-start.88 = (s32[16]{0:T(128)S(1)}, s32[16]{0:T(128)}, u32[]{:S(2)}) copy-start(s32[16]{0:T(128)} %param.10) | copy-start | bytes 196
  14.9 33.4 %all-to-all-start = ((bf16[8,2,64,512]{3,2,1,0:T(8,128)(2,1)}), bf16[8,2,64,512]{3,2,1,0:T(8,128)(2,1)S(1)}, u32[]{:S(2)}, u32[]{:S(2)}) async-start(bf16[8,2,64,512]{3,2,1,0:T(8,128)(2,1)} %stack.45), calls=%async_computation | async-start | bytes 2097152 | tf_op jit(solution)/shard_map/all_to_all | solution.py:15
  22.4 54.5 %all-gather.2.cloned.1.call-start = ((), (), s32[]{:S(2)}) async-start(), calls=%async_computation.5 | async-start | bytes 1179648 | tf_op jit(solution)/shard_map/all_gather | solution.py:180
  34.9 215.2 %all-reduce.7.cloned.1.call-start = ((), (), s32[]{:S(2)}) async-start(), calls=%async_computation.10 | async-start | bytes 4194304
  39.2 74.4 %copy-start.24 = (bf16[8,4,8,128]{3,2,1,0:T(8,128)(2,1)}, bf16[8,4,8,128]{3,2,1,0:T(8,128)(2,1)S(1)}, u32[]{:S(2)}) copy-start(bf16[8,4,8,128]{3,2,1,0:T(8,128)(2,1)S(1)} %get-tuple-element.29) | copy-start | bytes 196612
  39.2 81.0 %copy-start.22 = (bf16[8,4,8,128]{3,2,1,0:T(8,128)(2,1)}, bf16[8,4,8,128]{3,2,1,0:T(8,128)(2,1)S(1)}, u32[]{:S(2)}) copy-start(bf16[8,4,8,128]{3,2,1,0:T(8,128)(2,1)S(1)} %get-tuple-element.30) | copy-start | bytes 196612
  39.2 86.5 %copy-start.20 = (bf16[8,4,8,128]{3,2,1,0:T(8,128)(2,1)}, bf16[8,4,8,128]{3,2,1,0:T(8,128)(2,1)S(1)}, u32[]{:S(2)}) copy-start(bf16[8,4,8,128]{3,2,1,0:T(8,128)(2,1)S(1)} %get-tuple-element.31) | copy-start | bytes 196612
  39.3 92.0 %copy-start.19 = (bf16[8,4,8,128]{3,2,1,0:T(8,128)(2,1)}, bf16[8,4,8,128]{3,2,1,0:T(8,128)(2,1)S(1)}, u32[]{:S(2)}) copy-start(bf16[8,4,8,128]{3,2,1,0:T(8,128)(2,1)S(1)} %get-tuple-element.28) | copy-start | bytes 196612
  78.1 23.2 %copy-start.4 = (bf16[512,512]{1,0:T(8,128)(2,1)}, bf16[512,512]{1,0:T(8,128)(2,1)S(1)}, u32[]{:S(2)}) copy-start(bf16[512,512]{1,0:T(8,128)(2,1)S(1)} %get-tuple-element.14) | copy-start | bytes 1572868
  78.1 48.5 %copy-start.2 = (bf16[512,512]{1,0:T(8,128)(2,1)}, bf16[512,512]{1,0:T(8,128)(2,1)S(1)}, u32[]{:S(2)}) copy-start(bf16[512,512]{1,0:T(8,128)(2,1)S(1)} %get-tuple-element.15) | copy-start | bytes 1572868
  103.9 9.8 %copy-start.6 = (bf16[1,8,64,512]{3,2,0,1:T(8,128)(2,1)S(1)}, bf16[1,8,64,512]{3,2,0,1:T(8,128)(2,1)}, u32[]{:S(2)}) copy-start(bf16[1,8,64,512]{3,2,0,1:T(8,128)(2,1)} %get-tuple-element.13) | copy-start | bytes 1572868
  118.8 7.8 %copy-start.51 = (bf16[8,4,8,128]{3,2,1,0:T(8,128)(2,1)S(1)}, bf16[8,4,8,128]{3,2,1,0:T(8,128)(2,1)}, u32[]{:S(2)}) copy-start(bf16[8,4,8,128]{3,2,1,0:T(8,128)(2,1)} %get-tuple-element.36) | copy-start | bytes 196612
  123.1 8.1 %copy-start.84 = (f32[4,64]{1,0:T(4,128)}, f32[4,64]{1,0:T(4,128)S(1)}, u32[]{:S(2)}) copy-start(f32[4,64]{1,0:T(4,128)S(1)} %get-tuple-element.48) | copy-start | bytes 3076
  149.0 194.3 %reduce-scatter.5.cloned.1.call-start = ((), (), s32[]{:S(2)}) async-start(), calls=%async_computation.6 | async-start | bytes 4718592 | tf_op jit(solution)/shard_map/reduce_scatter | solution.py:226
  255.5 179.8 %reduce-scatter.9.cloned.1.call-start = ((), (), s32[]{:S(2)}) async-start(), calls=%async_computation.8 | async-start | bytes 4718592 | tf_op jit(solution)/shard_map/reduce_scatter | solution.py:229
  259.9 7.6 %copy-start.3 = (bf16[512,512]{1,0:T(8,128)(2,1)S(1)}, bf16[512,512]{1,0:T(8,128)(2,1)}, u32[]{:S(2)}) copy-start(bf16[512,512]{1,0:T(8,128)(2,1)} %copy-done.2) | copy-start | bytes 1572868
  259.9 199.1 %reduce-scatter.7.cloned.1.call-start = ((), (), s32[]{:S(2)}) async-start(), calls=%async_computation.7 | async-start | bytes 655360 | tf_op jit(solution)/shard_map/reduce_scatter | solution.py:237
  265.7 6.6 %copy-start.60 = (bf16[128,4,64]{0,2,1:T(8,128)(2,1)S(1)}, bf16[128,4,64]{0,2,1:T(8,128)(2,1)}, u32[]{:S(2)}) copy-start(bf16[128,4,64]{0,2,1:T(8,128)(2,1)} %get-tuple-element.69) | copy-start | bytes 196612
  265.7 6.7 %copy-start.61 = (bf16[128,4,64]{0,2,1:T(8,128)(2,1)S(1)}, bf16[128,4,64]{0,2,1:T(8,128)(2,1)}, u32[]{:S(2)}) copy-start(bf16[128,4,64]{0,2,1:T(8,128)(2,1)} %get-tuple-element.71) | copy-start | bytes 196612
  265.7 6.7 %copy-start.62 = (bf16[128,4,64]{0,2,1:T(8,128)(2,1)S(1)}, bf16[128,4,64]{0,2,1:T(8,128)(2,1)}, u32[]{:S(2)}) copy-start(bf16[128,4,64]{0,2,1:T(8,128)(2,1)} %get-tuple-element.73) | copy-start | bytes 196612
  343.3 139.7 %reduce-scatter.11.cloned.1.call-start = ((), (), s32[]{:S(2)}) async-start(), calls=%async_computation.9 | async-start | bytes 655360 | tf_op jit(solution)/shard_map/reduce_scatter | solution.py:240
  347.2 88.8 %copy-start.87 = (f32[128]{0:T(128)S(1)}, f32[128]{0:T(128)}, u32[]{:S(2)}) copy-start(f32[128]{0:T(128)} %multiply_multiply_fusion) | copy-start | bytes 1540
  (74 other events, 211.5 us)
Sparse Core Ops, SparseCore 0:
  35.0 41.7 all-gather.1
  149.1 100.9 all-reduce.6
  255.6 87.5 reduce-scatter.4
  346.7 88.5 reduce-scatter.8
  437.7 21.2 reduce-scatter.6
  461.3 21.6 reduce-scatter.10
